TPU v7x, 32 devices: a whole 2x2x4 slice. The times are simulated.
32 devices in a mesh: bond: 8 (over z, x), row: 4 (over y, core).
Axes of the slice: x: 2, y: 2, z: 4, core: 2. Of those that a mesh axis runs over, the one named last changes fastest.
Arguments:
- left_site: bfloat16 [16384, 1024], P(('bond', 'row')), may hold values from -6 to 6
- right_site: bfloat16 [8192, 2048], P(('bond', 'row')), may hold values from -0.1875 to 0.1875
- gate: float32 [4, 4], replicated, may hold values from -3 to 3
- omega: bfloat16 [2048, 1024], P(('bond', 'row')), may hold values from -0.125 to 0.125
Outputs:
- left_new: bfloat16 [16384, 1024], P(('bond', 'row'))
- right_new: bfloat16 [8192, 2048], P(('bond', 'row'))
- odd_pair: bfloat16 [16384, 2048], P(('bond', 'row'))
All inputs are finite; a program needn't handle non-finite values.
Results may differ from a plain program's by a relative error of at most 0.03.
Values may be sent and summed in bfloat16 or wider, within the bound.
A program may use at most 128 MiB of HBM per device.

v0:
```python
import math
import jax
import jax.numpy as jnp
from jax import lax
from jax.sharding import PartitionSpec as P


def from_behind(block, axis, distance):
    devices = range(lax.axis_size(axis))
    route = [(i - distance, i) for i in devices if i - distance in devices]
    return lax.ppermute(block, axis, route)


def shards(left_site, right_site, gate, omega):
    row_count = left_site.shape[0]
    bond_width = left_site.shape[1]
    kept_rank = omega.shape[1]
    columns = left_site
    product = jnp.dot(
        columns,
        lax.all_gather(right_site, "row", axis=0, tiled=True),
        preferred_element_type=jnp.float32,
    )
    mixed = jnp.einsum(
        "stuv,auvc->astc",
        gate.reshape(2, 2, 2, 2),
        product.reshape(row_count // 2, 2, 2, bond_width),
    )
    theta = mixed.reshape(row_count, 2 * bond_width).astype(jnp.bfloat16)
    columns = theta
    sketch = jnp.dot(
        columns,
        lax.all_gather(omega, ("bond", "row"), axis=0, tiled=True),
        preferred_element_type=jnp.float32,
    )
    local_gram = jnp.dot(sketch.T, sketch, precision=lax.Precision.HIGHEST)
    gram = lax.psum(local_gram, "row") / (2.0 * bond_width)
    diag_mean = jnp.trace(gram) / kept_rank
    lower = jnp.linalg.cholesky(gram + 0.01 * diag_mean * jnp.eye(kept_rank, dtype=jnp.float32))
    basis = lax.linalg.triangular_solve(
        lower, sketch, left_side=False, lower=True, transpose_a=True
    )
    left_new = basis.astype(jnp.bfloat16)
    right_scale = 1.0 / math.sqrt(2.0 * bond_width)
    own_rows = kept_rank // lax.axis_size("row")
    columns = left_new
    right_new = lax.psum_scatter(
        (
            lax.dot_general(
                columns, theta, (((0,), (0,)), ((), ())), preferred_element_type=jnp.float32
            )
            * right_scale
        ).astype(jnp.bfloat16),
        "row",
        scatter_dimension=0,
        tiled=True,
    )
    following = from_behind(left_new.reshape(row_count // 2, 2 * kept_rank), "bond", -1)
    right_view = right_new.reshape(2 * own_rows, bond_width)
    columns = right_view
    pair_sum = jnp.dot(
        columns,
        lax.all_gather(following, "row", axis=0, tiled=True),
        preferred_element_type=jnp.float32,
    )
    odd_pair = (pair_sum * (1.0 / math.sqrt(1.0 * bond_width))).astype(jnp.bfloat16)
    return (left_new, right_new, odd_pair)


def solution(mesh):
    placed = (P(("bond", "row"), None), P(("bond", "row"), None), P(), P(("bond", "row"), None))
    return jax.shard_map(
        shards,
        mesh=mesh,
        in_specs=placed,
        out_specs=(P(("bond", "row"), None), P(("bond", "row"), None), P(("bond", "row"), None)),
        check_vma=False,
    )
```

profile of v0, /device:TPU:0, one launch (start us, length us, event | category | flops | bytes accessed | tf_op | source)
XLA Modules:
  0.0 673.8 jit_solution(335509559467034745)
XLA Ops:
  9.5 37.3 %all-gather.4.cloned.1.call-done = bf16[1024,2048]{1,0:T(8,128)(2,1)} async-done(((bf16[256,2048]{1,0:T(8,128)(2,1)}), bf16[1024,2048]{1,0:T(8,128)(2,1)}) %all-gather.4.cloned.1.call-update) | async-done | bytes 4194320 | tf_op jit(solution)/shard_map/all_gather | solution.py:21
  46.8 5.8 fusion.68
  52.6 3.3 reshape.113
  55.9 3.6 bitcast_convert_fusion
  59.5 1.9 copy.58
  61.5 49.8 %all-gather.6.cloned.1.call-done = bf16[2048,1024]{1,0:T(8,128)(2,1)} async-done(((bf16[64,1024]{1,0:T(8,128)(2,1)}), bf16[2048,1024]{1,0:T(8,128)(2,1)}) %all-gather.6.cloned.1.call-update) | async-done | bytes 4194320 | tf_op jit(solution)/shard_map/all_gather | solution.py:33
  111.3 5.1 fusion.69
  116.4 8.4 %fusion.70 = f32[1024,1024]{0,1:T(8,128)} fusion(f32[512,1024]{1,0:T(8,128)S(1)} %fusion.69), kind=kOutput, calls=%fused_computation.167 | convolution fusion | flops 6442450944 | bytes 6291456 | tf_op jit(solution)/shard_map/dot_general | solution.py:36
  125.0 84.3 %all-reduce.3.cloned.1.call-done = f32[1024,1024]{0,1:T(8,128)} async-done(((f32[1024,1024]{0,1:T(8,128)}), f32[1024,1024]{0,1:T(8,128)}) %all-reduce.3.cloned.1.call-update) | async-done | bytes 4194320 | tf_op jit(solution)/shard_map/psum | solution.py:37
  209.3 2.9 select_reduce_fusion
  212.9 5.0 select_add_fusion
  217.9 5.5 copy.29
  223.4 4.5 fusion
  227.9 1.9 copy-done.3
  229.8 11.7 %cholesky.222 = f32[128,128]{1,0:T(8,128)S(1)} custom-call(f32[128,128]{1,0:T(8,128)S(1)} %cholesky.577), custom_call_target="Cholesky" | custom-call | tf_op jit(solution)/shard_map/jit(cholesky)/cholesky | solution.py:39
  241.7 9.8 %custom-call.62 = f32[1,128,128]{1,2,0:T(8,128)S(1)} custom-call(f32[1,128,128]{2,1,0:T(8,128)S(1)} %get-tuple-element.73), custom_call_target="InvertDiagBlocksLowerTriangular" | custom-call | tf_op jit(solution)/shard_map/jit(cholesky)/cholesky | solution.py:39
  251.5 1.5 fusion.27
  253.0 1.5 convolution_subtract_fusion
  254.8 11.7 %cholesky.243 = f32[128,128]{1,0:T(8,128)S(1)} custom-call(f32[128,128]{1,0:T(8,128)S(1)} %cholesky.581), custom_call_target="Cholesky" | custom-call | tf_op jit(solution)/shard_map/jit(cholesky)/cholesky | solution.py:39
  267.0 9.8 %custom-call.63 = f32[1,128,128]{1,2,0:T(8,128)S(1)} custom-call(f32[1,128,128]{2,1,0:T(8,128)S(1)} %get-tuple-element.71), custom_call_target="InvertDiagBlocksLowerTriangular" | custom-call | tf_op jit(solution)/shard_map/jit(cholesky)/cholesky | solution.py:39
  278.0 2.0 copy-done.2
  279.9 2.4 convolution_subtract_fusion.1
  282.4 11.7 %cholesky.466 = f32[128,128]{1,0:T(8,128)S(1)} custom-call(f32[128,128]{1,0:T(8,128)S(1)} %cholesky.586), custom_call_target="Cholesky" | custom-call | tf_op jit(solution)/shard_map/jit(cholesky)/cholesky | solution.py:39
  294.9 9.8 %custom-call.64 = f32[1,128,128]{1,2,0:T(8,128)S(1)} custom-call(f32[1,128,128]{2,1,0:T(8,128)S(1)} %get-tuple-element.69), custom_call_target="InvertDiagBlocksLowerTriangular" | custom-call | tf_op jit(solution)/shard_map/jit(cholesky)/cholesky | solution.py:39
  305.9 3.3 convolution_subtract_fusion.2
  309.3 11.7 %cholesky.485 = f32[128,128]{1,0:T(8,128)S(1)} custom-call(f32[128,128]{1,0:T(8,128)S(1)} %cholesky.591), custom_call_target="Cholesky" | custom-call | tf_op jit(solution)/shard_map/jit(cholesky)/cholesky | solution.py:39
  321.7 9.8 %custom-call.65 = f32[1,128,128]{1,2,0:T(8,128)S(1)} custom-call(f32[1,128,128]{2,1,0:T(8,128)S(1)} %get-tuple-element.67), custom_call_target="InvertDiagBlocksLowerTriangular" | custom-call | tf_op jit(solution)/shard_map/jit(cholesky)/cholesky | solution.py:39
  332.7 3.2 convolution_subtract_fusion.10
  335.9 12.1 %cholesky.504 = f32[128,128]{1,0:T(8,128)S(1)} custom-call(f32[128,128]{1,0:T(8,128)S(1)} %cholesky.596), custom_call_target="Cholesky" | custom-call | tf_op jit(solution)/shard_map/jit(cholesky)/cholesky | solution.py:39
  348.7 9.8 %custom-call.66 = f32[1,128,128]{1,2,0:T(8,128)S(1)} custom-call(f32[1,128,128]{2,1,0:T(8,128)S(1)} %get-tuple-element.65), custom_call_target="InvertDiagBlocksLowerTriangular" | custom-call | tf_op jit(solution)/shard_map/jit(cholesky)/cholesky | solution.py:39
  359.7 3.1 convolution_subtract_fusion.11
  362.8 11.7 %cholesky.524 = f32[128,128]{1,0:T(8,128)S(1)} custom-call(f32[128,128]{1,0:T(8,128)S(1)} %cholesky.601), custom_call_target="Cholesky" | custom-call | tf_op jit(solution)/shard_map/jit(cholesky)/cholesky | solution.py:39
  375.2 9.8 %custom-call.67 = f32[1,128,128]{1,2,0:T(8,128)S(1)} custom-call(f32[1,128,128]{2,1,0:T(8,128)S(1)} %get-tuple-element.63), custom_call_target="InvertDiagBlocksLowerTriangular" | custom-call | tf_op jit(solution)/shard_map/jit(cholesky)/cholesky | solution.py:39
  386.0 2.8 convolution_subtract_fusion.12
  388.9 11.7 %cholesky.544 = f32[128,128]{1,0:T(8,128)S(1)} custom-call(f32[128,128]{1,0:T(8,128)S(1)} %cholesky.606), custom_call_target="Cholesky" | custom-call | tf_op jit(solution)/shard_map/jit(cholesky)/cholesky | solution.py:39
  401.4 9.8 %custom-call.68 = f32[1,128,128]{1,2,0:T(8,128)S(1)} custom-call(f32[1,128,128]{2,1,0:T(8,128)S(1)} %get-tuple-element.61), custom_call_target="InvertDiagBlocksLowerTriangular" | custom-call | tf_op jit(solution)/shard_map/jit(cholesky)/cholesky | solution.py:39
  412.1 2.1 convolution_subtract_fusion.13
  414.2 11.7 %cholesky.562 = f32[128,128]{1,0:T(8,128)S(1)} custom-call(f32[128,128]{1,0:T(8,128)S(1)} %convolution_subtract_fusion.13), custom_call_target="Cholesky" | custom-call | tf_op jit(solution)/shard_map/jit(cholesky)/cholesky | solution.py:39
  436.4 4.8 select_select_fusion
  441.3 28.6 %while.1 = (s32[]{:T(128)}, f32[1024,1024]{0,1:T(8,128)}, s32[8,2]{0,1:T(2,128)S(1)}, f32[8,128,128]{2,1,0:T(8,128)}, s32[]{:T(128)}) while((s32[]{:T(128)}, f32[1024,1024]{0,1:T(8,128)}, s32[8,2]{0,1:T(2,128)S(1)}, f32[8,128,128]{2,1,0:T(8,128)}, s32[]{:T(128)}) %tuple.57), condition=%wide.while_cond, body=%wide.while_body.sunk | while | flops 2 | bytes 393329 | solution.py:40
  441.9 2.2 dynamic-slice.7
  445.5 2.2 dynamic-slice.7
  449.0 2.2 dynamic-slice.7
  452.6 2.2 dynamic-slice.7
  456.2 2.2 dynamic-slice.7
  459.8 2.2 dynamic-slice.7
  463.4 2.2 dynamic-slice.7
  467.0 2.2 dynamic-slice.7
  469.9 80.2 %custom-call.69 = f32[8,128,128]{1,2,0:T(8,128)} custom-call(f32[8,128,128]{2,1,0:T(8,128)} %get-tuple-element.10), custom_call_target="InvertDiagBlocksLowerTriangular" | custom-call | tf_op jit(solution)/shard_map/triangular_solve | solution.py:40
  550.1 1.4 constant_dynamic-update-slice_fusion.17
  551.5 1.4 convolution_subtract_fusion.6
  552.9 1.3 constant_dynamic-update-slice_fusion.16
  554.2 1.9 convolution_subtract_fusion.5
  556.6 2.4 convolution_subtract_fusion.8
  559.5 2.8 convolution_subtract_fusion.9
  562.7 3.2 convolution_subtract_fusion.4
  566.3 3.8 convolution_subtract_fusion.7
  570.8 4.1 convolution_subtract_fusion.3
  575.3 4.3 multiply_convert_fusion
  582.0 25.2 %collective-permute-done = bf16[256,2048]{1,0:T(8,128)(2,1)S(1)} collective-permute-done((bf16[256,2048]{1,0:T(8,128)(2,1)S(1)}, bf16[256,2048]{1,0:T(8,128)(2,1)S(1)}, u32[]{:S(2)}, u32[]{:S(2)}) %collective-permute-start) | collective-permute-done | bytes 1048608 | tf_op jit(solution)/shard_map/ppermute | solution.py:11
  608.2 16.4 %reduce-scatter.2.cloned.1.call-done = bf16[256,2048]{1,0:T(8,128)(2,1)} async-done(((bf16[1024,2048]{1,0:T(8,128)(2,1)}), bf16[256,2048]{1,0:T(8,128)(2,1)}) %reduce-scatter.2.cloned.1.call-update) | async-done | bytes 1048592 | tf_op jit(solution)/shard_map/reduce_scatter | solution.py:47
  624.5 1.5 reshape.89
  626.0 35.0 %all-gather.8.cloned.1.call-done = bf16[1024,2048]{1,0:T(8,128)(2,1)} async-done(((bf16[256,2048]{1,0:T(8,128)(2,1)}), bf16[1024,2048]{1,0:T(8,128)(2,1)}) %all-gather.8.cloned.1.call-update) | async-done | bytes 4194320 | tf_op jit(solution)/shard_map/all_gather | solution.py:63
  661.0 5.8 multiply_convert_fusion.1
  (115 shorter events, 36.0 us)
Async XLA Ops:
  7.2 39.6 %copy-start = (bf16[512,1024]{1,0:T(8,128)(2,1)S(1)}, bf16[512,1024]{1,0:T(8,128)(2,1)}, u32[]{:S(2)}) copy-start(bf16[512,1024]{1,0:T(8,128)(2,1)} %param.4) | copy-start | bytes 3145732
  7.2 39.6 %all-gather.4.cloned.1.call-start = ((), (), s32[]{:S(2)}) async-start(), calls=%async_computation.1 | async-start | bytes 5242880 | tf_op jit(solution)/shard_map/all_gather | solution.py:21
  7.9 103.4 %all-gather.6.cloned.1.call-start = ((), (), s32[]{:S(2)}) async-start(), calls=%async_computation.2 | async-start | bytes 4325376 | tf_op jit(solution)/shard_map/all_gather | solution.py:33
  8.7 200.6 %all-reduce.3.cloned.1.call-start = ((), (), s32[]{:S(2)}) async-start(), calls=%async_computation.3 | async-start | bytes 8388608 | tf_op jit(solution)/shard_map/psum | solution.py:37
  124.9 499.6 %reduce-scatter.2.cloned.1.call-start = ((), (), s32[]{:S(2)}) async-start(), calls=%async_computation.4 | async-start | bytes 5242880 | tf_op jit(solution)/shard_map/reduce_scatter | solution.py:47
  227.9 1.9 copy-start.3
  278.0 2.0 copy-start.2
  550.1 6.0 copy-start.7
  565.9 9.4 %copy-start.5 = (bf16[64,8,2,1024]{3,1,2,0:T(8,128)(2,1)S(1)}, bf16[64,8,2,1024]{3,1,2,0:T(8,128)(2,1)}, u32[]{:S(2)}) copy-start(bf16[64,8,2,1024]{3,1,2,0:T(8,128)(2,1)} %copy.58) | copy-start | bytes 6291460
  579.7 81.3 %all-gather.8.cloned.1.call-start = ((), (), s32[]{:S(2)}) async-start(), calls=%async_computation.5 | async-start | bytes 5242880 | tf_op jit(solution)/shard_map/all_gather | solution.py:63
  580.3 86.6 %copy-start.4 = (bf16[512,1024]{1,0:T(8,128)(2,1)}, bf16[512,1024]{1,0:T(8,128)(2,1)S(1)}, u32[]{:S(2)}) copy-start(bf16[512,1024]{1,0:T(8,128)(2,1)S(1)} %copy.47) | copy-start | bytes 3145732
  580.7 26.5 %collective-permute-start = (bf16[256,2048]{1,0:T(8,128)(2,1)S(1)}, bf16[256,2048]{1,0:T(8,128)(2,1)S(1)}, u32[]{:S(2)}, u32[]{:S(2)}) collective-permute-start(bf16[256,2048]{1,0:T(8,128)(2,1)S(1)} %convert_element_type.28), channel_id=1, source_target_pairs={{4,0},{8,4},{12,8},{16,12},{20,16},{24,20},{28,24},{5,1},{9,5},{13... | collective-permute-start | bytes 3145736 | tf_op jit(solution)/shard_map/ppermute | solution.py:11
  607.2 1.0 copy-start.6
  624.5 42.3 %copy-start.1 = (bf16[512,1024]{1,0:T(8,128)(2,1)S(1)}, bf16[512,1024]{1,0:T(8,128)(2,1)}, u32[]{:S(2)}) copy-start(bf16[512,1024]{1,0:T(8,128)(2,1)} %param.4) | copy-start | bytes 3145732
Sparse Core Ops, SparseCore 0:
  9.5 37.1 all-gather.3
  49.6 61.6 all-gather.5
  125.0 84.2 all-reduce.2
  579.8 44.6 reduce-scatter.1
  626.5 34.4 all-gather.7
where the time goes:
time: 683 us; the launch traced here: 674 us
  other arithmetic  265 us (39%)
  waiting for transfers between devices  249 us (36%)
  matrix products  84.2 us (12%)
  local copies, waits for them, and re-layouts  53.1 us (8%)
  between operations  20.4 us (3%)
    another operation x30, other arithmetic, shards(): jnp.linalg.cholesky(gram + 0.01 * diag_mean * jnp.eye(kept_rank, dtype=jn...  168 us
    another operation x3, other arithmetic, shards(): lax.linalg.triangular_solve(lower, sketch, left_side=False, lower=True, t...  85.1 us
    psum x1, waiting for transfers between devices, shards(): gram = lax.psum(local_gram, 'row') / (2.0 * bond_width)  84.3 us
    all_gather x1, waiting for transfers between devices, shards(): lax.all_gather(omega, ('bond', 'row'), axis=0, tiled=True)  49.8 us
    all_gather x1, waiting for transfers between devices, shards(): lax.all_gather(right_site, 'row', axis=0, tiled=True)  37.3 us
    all_gather x1, waiting for transfers between devices, shards(): lax.all_gather(following, 'row', axis=0, tiled=True)  35 us
    another operation x40, local copies, waits for them, and re-layouts  28.5 us
    another operation x14, matrix products, shards(): jnp.linalg.cholesky(gram + 0.01 * diag_mean * jnp.eye(kept_rank, dtype=jn...  25.9 us
  transfers between devices with their start and end apart: 6, of which 6 were waited for; matrix products, arithmetic and copies ran while one was open for 3% of the time, Pallas kernels for 0%

commit v1 on v0

--- a/solution.py
+++ b/solution.py
@@ -34,7 +34,7 @@
         preferred_element_type=jnp.float32,
     )
     local_gram = jnp.dot(sketch.T, sketch, precision=lax.Precision.HIGHEST)
-    gram = lax.psum(local_gram, "row") / (2.0 * bond_width)
+    gram = jnp.sum(lax.all_gather(local_gram, "row"), axis=0) / (2.0 * bond_width)
     diag_mean = jnp.trace(gram) / kept_rank
     lower = jnp.linalg.cholesky(gram + 0.01 * diag_mean * jnp.eye(kept_rank, dtype=jnp.float32))
     basis = lax.linalg.triangular_solve(

time: 683 us -> 715 us (1.047)
  other arithmetic: 265 us -> 286 us
  waiting for transfers between devices: 249 us -> 268 us
    all_gather x0 -> x1, waiting for transfers between devices: none -> 105 us  [shards(): lax.all_gather(local_gram, 'row')]
    psum x1 -> x0, waiting for transfers between devices: 84.3 us -> none  [shards(): gram = lax.psum(local_gram, 'row') / (2.0 * bond_width)]
    another operation x30, other arithmetic: 168 us -> 181 us  [shards(): jnp.linalg.cholesky(gram + 0.01 * diag_mean * jnp.eye(kept_rank, dtype=jn...]
    reduce_sum x0 -> x1, other arithmetic: none -> 10.3 us  [shards(): jnp.sum(lax.all_gather(local_gram, 'row'), axis=0) / (2.0 * bond_width)]
    another operation x40 -> x24, local copies, waits for them, and re-layouts: 28.5 us -> 27.7 us
where the time goes in v1:
time: 715 us; the launch traced here: 706 us
  other arithmetic  286 us (40%)
  waiting for transfers between devices  268 us (37%)
  matrix products  81.2 us (11%)
  local copies, waits for them, and re-layouts  49.4 us (7%)
  between operations  20 us (3%)
    another operation x30, other arithmetic, shards(): jnp.linalg.cholesky(gram + 0.01 * diag_mean * jnp.eye(kept_rank, dtype=jn...  181 us
    all_gather x1, waiting for transfers between devices, shards(): lax.all_gather(local_gram, 'row')  105 us
    another operation x3, other arithmetic, shards(): lax.linalg.triangular_solve(lower, sketch, left_side=False, lower=True, t...  84.4 us
    all_gather x1, waiting for transfers between devices, shards(): lax.all_gather(omega, ('bond', 'row'), axis=0, tiled=True)  49.8 us
    all_gather x1, waiting for transfers between devices, shards(): lax.all_gather(right_site, 'row', axis=0, tiled=True)  37.3 us
    all_gather x1, waiting for transfers between devices, shards(): lax.all_gather(following, 'row', axis=0, tiled=True)  35 us
    another operation x24, local copies, waits for them, and re-layouts  27.7 us
    ppermute x1, waiting for transfers between devices, from_behind(): return lax.ppermute(block, axis, route)  25.9 us
  transfers between devices with their start and end apart: 6, of which 6 were waited for; matrix products, arithmetic and copies ran while one was open for 3% of the time, Pallas kernels for 0%

profile of v1, /device:TPU:0, one launch (start us, length us, event | category | flops | bytes accessed | tf_op | source)
XLA Modules:
  0.0 706.2 jit_solution(14047227689214703211)
XLA Ops:
  9.5 37.3 %all-gather.6.cloned.1.call-done = bf16[1024,2048]{1,0:T(8,128)(2,1)} async-done(((bf16[256,2048]{1,0:T(8,128)(2,1)}), bf16[1024,2048]{1,0:T(8,128)(2,1)}) %all-gather.6.cloned.1.call-update) | async-done | bytes 4194320 | tf_op jit(solution)/shard_map/all_gather | solution.py:21
  46.8 5.8 fusion.67
  52.6 3.3 reshape.114
  55.9 3.6 bitcast_convert_fusion
  59.5 1.9 copy.16
  61.5 49.8 %all-gather.8.cloned.1.call-done = bf16[2048,1024]{1,0:T(8,128)(2,1)} async-done(((bf16[64,1024]{1,0:T(8,128)(2,1)}), bf16[2048,1024]{1,0:T(8,128)(2,1)}) %all-gather.8.cloned.1.call-update) | async-done | bytes 4194320 | tf_op jit(solution)/shard_map/all_gather | solution.py:33
  111.3 5.1 fusion.68
  116.4 8.3 %fusion.69 = f32[1024,1024]{1,0:T(8,128)} fusion(f32[512,1024]{1,0:T(8,128)S(1)} %fusion.68), kind=kOutput, calls=%fused_computation.167 | convolution fusion | flops 6442450944 | bytes 6291456 | tf_op jit(solution)/shard_map/dot_general | solution.py:36
  125.1 104.5 %all-gather.12.cloned.1.call-done = f32[4096,1024]{1,0:T(8,128)} async-done(((f32[1024,1024]{1,0:T(8,128)}), f32[4096,1024]{1,0:T(8,128)}) %all-gather.12.cloned.1.call-update) | async-done | bytes 16777232 | tf_op jit(solution)/shard_map/all_gather | solution.py:37
  229.6 10.3 %reduce_sum.19 = f32[1024,1024]{1,0:T(8,128)} reduce(f32[4,1024,1024]{2,1,0:T(8,128)} %bitcast.125, f32[]{:T(128)} %constant.277.clone.1), dimensions={0}, to_apply=%region_0.0 | reduce | flops 3145728 | bytes 20971524 | tf_op jit(solution)/shard_map/reduce_sum | solution.py:37
  239.9 5.6 select_reduce_fusion
  245.5 5.3 copy.11
  251.4 4.5 add_multiply_fusion
  255.9 1.9 copy-done.2
  257.8 11.7 %cholesky.222 = f32[128,128]{1,0:T(8,128)S(1)} custom-call(f32[128,128]{1,0:T(8,128)S(1)} %cholesky.577), custom_call_target="Cholesky" | custom-call | tf_op jit(solution)/shard_map/jit(cholesky)/cholesky | solution.py:39
  269.5 2.5 cholesky.254
  272.0 9.8 %custom-call.62 = f32[1,128,128]{1,2,0:T(8,128)S(1)} custom-call(f32[1,128,128]{2,1,0:T(8,128)S(1)} %get-tuple-element.75), custom_call_target="InvertDiagBlocksLowerTriangular" | custom-call | tf_op jit(solution)/shard_map/jit(cholesky)/cholesky | solution.py:39
  281.9 2.4 constant_dynamic-update-slice_fusion.32
  284.2 1.5 convolution_subtract_fusion
  285.8 20.4 %cholesky.243 = f32[128,128]{1,0:T(8,128)S(1)} custom-call(f32[128,128]{1,0:T(8,128)S(1)} %cholesky.581), custom_call_target="Cholesky" | custom-call | tf_op jit(solution)/shard_map/jit(cholesky)/cholesky | solution.py:39
  306.8 9.8 %custom-call.63 = f32[1,128,128]{1,2,0:T(8,128)S(1)} custom-call(f32[1,128,128]{2,1,0:T(8,128)S(1)} %get-tuple-element.72), custom_call_target="InvertDiagBlocksLowerTriangular" | custom-call | tf_op jit(solution)/shard_map/jit(cholesky)/cholesky | solution.py:39
  317.9 2.1 convolution_subtract_fusion.1
  320.0 11.7 %cholesky.466 = f32[128,128]{1,0:T(8,128)S(1)} custom-call(f32[128,128]{1,0:T(8,128)S(1)} %cholesky.586), custom_call_target="Cholesky" | custom-call | tf_op jit(solution)/shard_map/jit(cholesky)/cholesky | solution.py:39
  333.0 9.8 %custom-call.64 = f32[1,128,128]{1,2,0:T(8,128)S(1)} custom-call(f32[1,128,128]{2,1,0:T(8,128)S(1)} %get-tuple-element.69), custom_call_target="InvertDiagBlocksLowerTriangular" | custom-call | tf_op jit(solution)/shard_map/jit(cholesky)/cholesky | solution.py:39
  343.9 2.3 convolution_subtract_fusion.2
  346.3 11.9 %cholesky.485 = f32[128,128]{1,0:T(8,128)S(1)} custom-call(f32[128,128]{1,0:T(8,128)S(1)} %cholesky.591), custom_call_target="Cholesky" | custom-call | tf_op jit(solution)/shard_map/jit(cholesky)/cholesky | solution.py:39
  359.5 9.8 %custom-call.65 = f32[1,128,128]{1,2,0:T(8,128)S(1)} custom-call(f32[1,128,128]{2,1,0:T(8,128)S(1)} %get-tuple-element.66), custom_call_target="InvertDiagBlocksLowerTriangular" | custom-call | tf_op jit(solution)/shard_map/jit(cholesky)/cholesky | solution.py:39
  370.4 2.3 convolution_subtract_fusion.10
  372.8 11.7 %cholesky.504 = f32[128,128]{1,0:T(8,128)S(1)} custom-call(f32[128,128]{1,0:T(8,128)S(1)} %cholesky.596), custom_call_target="Cholesky" | custom-call | tf_op jit(solution)/shard_map/jit(cholesky)/cholesky | solution.py:39
  385.8 10.2 %custom-call.66 = f32[1,128,128]{1,2,0:T(8,128)S(1)} custom-call(f32[1,128,128]{2,1,0:T(8,128)S(1)} %get-tuple-element.63), custom_call_target="InvertDiagBlocksLowerTriangular" | custom-call | tf_op jit(solution)/shard_map/jit(cholesky)/cholesky | solution.py:39
  397.0 2.3 convolution_subtract_fusion.11
  399.3 11.7 %cholesky.524 = f32[128,128]{1,0:T(8,128)S(1)} custom-call(f32[128,128]{1,0:T(8,128)S(1)} %cholesky.601), custom_call_target="Cholesky" | custom-call | tf_op jit(solution)/shard_map/jit(cholesky)/cholesky | solution.py:39
  412.3 9.8 %custom-call.67 = f32[1,128,128]{1,2,0:T(8,128)S(1)} custom-call(f32[1,128,128]{2,1,0:T(8,128)S(1)} %get-tuple-element.60), custom_call_target="InvertDiagBlocksLowerTriangular" | custom-call | tf_op jit(solution)/shard_map/jit(cholesky)/cholesky | solution.py:39
  423.0 2.0 convolution_subtract_fusion.12
  425.1 11.9 %cholesky.544 = f32[128,128]{1,0:T(8,128)S(1)} custom-call(f32[128,128]{1,0:T(8,128)S(1)} %cholesky.606), custom_call_target="Cholesky" | custom-call | tf_op jit(solution)/shard_map/jit(cholesky)/cholesky | solution.py:39
  438.2 9.8 %custom-call.68 = f32[1,128,128]{1,2,0:T(8,128)S(1)} custom-call(f32[1,128,128]{2,1,0:T(8,128)S(1)} %get-tuple-element.57), custom_call_target="InvertDiagBlocksLowerTriangular" | custom-call | tf_op jit(solution)/shard_map/jit(cholesky)/cholesky | solution.py:39
  448.8 1.8 convolution_subtract_fusion.13
  450.6 11.7 %cholesky.562 = f32[128,128]{1,0:T(8,128)S(1)} custom-call(f32[128,128]{1,0:T(8,128)S(1)} %convolution_subtract_fusion.13), custom_call_target="Cholesky" | custom-call | tf_op jit(solution)/shard_map/jit(cholesky)/cholesky | solution.py:39
  469.2 4.8 select_select_fusion
  474.0 27.7 %while.1 = (s32[]{:T(128)}, f32[1024,1024]{1,0:T(8,128)}, s32[8,2]{0,1:T(2,128)S(1)}, f32[8,128,128]{2,1,0:T(8,128)}, s32[]{:T(128)}) while((s32[]{:T(128)}, f32[1024,1024]{1,0:T(8,128)}, s32[8,2]{0,1:T(2,128)S(1)}, f32[8,128,128]{2,1,0:T(8,128)}, s32[]{:T(128)}) %tuple.64), condition=%wide.while_cond, body=%wide.while_body.sunk | while | flops 2 | bytes 132705 | solution.py:40
  474.6 2.9 bitcast_dynamic-update-slice_fusion.2
  478.1 2.9 bitcast_dynamic-update-slice_fusion.2
  481.5 2.9 bitcast_dynamic-update-slice_fusion.2
  485.0 2.9 bitcast_dynamic-update-slice_fusion.2
  488.5 2.9 bitcast_dynamic-update-slice_fusion.2
  492.0 2.9 bitcast_dynamic-update-slice_fusion.2
  495.4 2.9 bitcast_dynamic-update-slice_fusion.2
  498.9 2.8 bitcast_dynamic-update-slice_fusion.2
  501.7 79.6 %custom-call.69 = f32[8,128,128]{1,2,0:T(8,128)S(1)} custom-call(f32[8,128,128]{2,1,0:T(8,128)} %get-tuple-element.10), custom_call_target="InvertDiagBlocksLowerTriangular" | custom-call | tf_op jit(solution)/shard_map/triangular_solve | solution.py:40
  582.1 1.5 convolution_subtract_fusion.6
  583.6 1.3 constant_dynamic-update-slice_fusion.16
  584.9 1.9 convolution_subtract_fusion.5
  586.8 1.3 constant_dynamic-update-slice_fusion.15
  588.1 2.4 convolution_subtract_fusion.8
  591.0 2.8 convolution_subtract_fusion.9
  594.2 3.2 convolution_subtract_fusion.4
  597.9 3.8 convolution_subtract_fusion.7
  602.1 4.3 convolution_subtract_fusion.3
  607.9 4.3 multiply_convert_fusion
  615.7 25.9 %collective-permute-done = bf16[256,2048]{1,0:T(8,128)(2,1)S(1)} collective-permute-done((bf16[256,2048]{1,0:T(8,128)(2,1)S(1)}, bf16[256,2048]{1,0:T(8,128)(2,1)S(1)}, u32[]{:S(2)}, u32[]{:S(2)}) %collective-permute-start) | collective-permute-done | bytes 1048608 | tf_op jit(solution)/shard_map/ppermute | solution.py:11
  642.6 14.4 %reduce-scatter.2.cloned.1.call-done = bf16[256,2048]{1,0:T(8,128)(2,1)} async-done(((bf16[1024,2048]{1,0:T(8,128)(2,1)}), bf16[256,2048]{1,0:T(8,128)(2,1)}) %reduce-scatter.2.cloned.1.call-update) | async-done | bytes 1048592 | tf_op jit(solution)/shard_map/reduce_scatter | solution.py:47
  656.9 1.5 reshape.89
  658.4 35.0 %all-gather.10.cloned.1.call-done = bf16[1024,2048]{1,0:T(8,128)(2,1)} async-done(((bf16[256,2048]{1,0:T(8,128)(2,1)}), bf16[1024,2048]{1,0:T(8,128)(2,1)}) %all-gather.10.cloned.1.call-update) | async-done | bytes 4194320 | tf_op jit(solution)/shard_map/all_gather | solution.py:63
  693.4 5.8 multiply_convert_fusion.1
  (86 shorter events, 31.3 us)
Async XLA Ops:
  7.2 39.6 %copy-start = (bf16[512,1024]{1,0:T(8,128)(2,1)S(1)}, bf16[512,1024]{1,0:T(8,128)(2,1)}, u32[]{:S(2)}) copy-start(bf16[512,1024]{1,0:T(8,128)(2,1)} %param.4) | copy-start | bytes 3145732
  7.2 39.6 %all-gather.6.cloned.1.call-start = ((), (), s32[]{:S(2)}) async-start(), calls=%async_computation.1 | async-start | bytes 5242880 | tf_op jit(solution)/shard_map/all_gather | solution.py:21
  7.9 103.4 %all-gather.8.cloned.1.call-start = ((), (), s32[]{:S(2)}) async-start(), calls=%async_computation.2 | async-start | bytes 4325376 | tf_op jit(solution)/shard_map/all_gather | solution.py:33
  8.7 220.9 %all-gather.12.cloned.1.call-start = ((), (), s32[]{:S(2)}) async-start(), calls=%async_computation.5 | async-start | bytes 20971520 | tf_op jit(solution)/shard_map/all_gather | solution.py:37
  124.8 532.2 %reduce-scatter.2.cloned.1.call-start = ((), (), s32[]{:S(2)}) async-start(), calls=%async_computation.3 | async-start | bytes 5242880 | tf_op jit(solution)/shard_map/reduce_scatter | solution.py:47
  255.9 1.9 copy-start.2
  581.3 0.8 copy-start.8
  582.1 8.4 %copy-start.9 = (f32[8,128,128]{1,2,0:T(8,128)S(1)}, f32[8,128,128]{1,2,0:T(8,128)}, u32[]{:S(2)}) copy-start(f32[8,128,128]{1,2,0:T(8,128)} %copy-done.8) | copy-start | bytes 1572868
  597.5 10.4 %copy-start.4 = (bf16[64,8,2,1024]{3,1,2,0:T(8,128)(2,1)S(1)}, bf16[64,8,2,1024]{3,1,2,0:T(8,128)(2,1)}, u32[]{:S(2)}) copy-start(bf16[64,8,2,1024]{3,1,2,0:T(8,128)(2,1)} %copy.16) | copy-start | bytes 6291460
  606.9 1.0 copy-start.5
  612.2 1.2 copy-start.6
  612.2 81.2 %all-gather.10.cloned.1.call-start = ((), (), s32[]{:S(2)}) async-start(), calls=%async_computation.4 | async-start | bytes 5242880 | tf_op jit(solution)/shard_map/all_gather | solution.py:63
  613.9 85.3 %copy-start.3 = (bf16[512,1024]{1,0:T(8,128)(2,1)}, bf16[512,1024]{1,0:T(8,128)(2,1)S(1)}, u32[]{:S(2)}) copy-start(bf16[512,1024]{1,0:T(8,128)(2,1)S(1)} %copy.13) | copy-start | bytes 3145732
  614.4 27.2 %collective-permute-start = (bf16[256,2048]{1,0:T(8,128)(2,1)S(1)}, bf16[256,2048]{1,0:T(8,128)(2,1)S(1)}, u32[]{:S(2)}, u32[]{:S(2)}) collective-permute-start(bf16[256,2048]{1,0:T(8,128)(2,1)S(1)} %convert_element_type.28), channel_id=1, source_target_pairs={{4,0},{8,4},{12,8},{16,12},{20,16},{24,20},{28,24},{5,1},{9,5},{13... | collective-permute-start | bytes 3145736 | tf_op jit(solution)/shard_map/ppermute | solution.py:11
  641.6 1.0 copy-start.7
  656.9 42.3 %copy-start.1 = (bf16[512,1024]{1,0:T(8,128)(2,1)S(1)}, bf16[512,1024]{1,0:T(8,128)(2,1)}, u32[]{:S(2)}) copy-start(bf16[512,1024]{1,0:T(8,128)(2,1)} %param.4) | copy-start | bytes 3145732
Sparse Core Ops, SparseCore 0:
  9.5 37.1 all-gather.5
  49.6 61.6 all-gather.7
  124.9 104.6 all-gather.11
  612.3 44.5 reduce-scatter.1
  658.9 34.4 all-gather.9
